TPU v7x, 32 devices: a whole 2x2x4 slice. The times are simulated.
32 devices in a mesh: gx: 4 (over z), gy: 8 (over y, x, core).
Axes of the slice: x: 2, y: 2, z: 4, core: 2. Of those that a mesh axis runs over, the one named last changes fastest.
Arguments:
- forcing: float32 [4, 512, 2048], P(None, ('gx', 'gy')), may hold values from -6 to 6
- ice_state: float32 [2, 512, 2048], P(None, ('gx', 'gy')), may hold values from 0.3 to 3, as said below
- velocity: float32 [2, 512, 2048], P(None, ('gx', 'gy')), may hold values from -4 to 4
- stress: float32 [3, 512, 2048], P(None, ('gx', 'gy')), may hold values from -4 to 4
- ice_mask: int32 [512, 2048], P(('gx', 'gy')), may hold values from 0 to 2, as said below
Outputs:
- ice_velocity: float32 [2, 512, 2048], P(None, ('gx', 'gy'))
- ice_stress: float32 [3, 512, 2048], P(None, ('gx', 'gy'))
- ocean_stress: float32 [2, 512, 2048], P(None, ('gx', 'gy'))
Inputs may be any that keep to these rules, and one draw needn't show every extreme that they name: `ice_state`: row 0 lies in 0.7 to 1, row 1 in 0.3 to 3. `ice_mask`: 0 marks land, 1 open water, 2 ice-covered cells.
All inputs are finite; a program needn't handle non-finite values.
Results may differ from a plain program's by a relative error of at most 0.00002.
Values sent between devices are 32-bit elements; how exact they have to be, the bound alone decides.
A program may use at most 128 MiB of HBM per device.

v0:
```python
import functools
import math

import jax
import jax.numpy as jnp
from jax import lax
from jax.experimental import pallas as pl
from jax.experimental.pallas import tpu as pltpu
from jax.sharding import PartitionSpec as P

ITERS = 4
C_STAR = 20.0
DELTA_MIN = 0.05
ALPHA_EVP = 30.0
BETA_EVP = 30.0
DRAG_COEF = 0.5
SPEED_FLOOR = 0.05
CORIOLIS_MAX = 0.5

MESH = pl.DeviceIdType.MESH
LANES = 128
SUB = 8
OFF = 7
CH = 2
VEL_HALO = 6
REST_HALO = 5
STRESS_REACH = (5, 4, 2, 1)
VEL_REACH = (5, 3, 2, 0)


def loop(lo, hi, body):
    turns = (hi - lo) // CH

    def turn(t, carry):
        body(lo + t * CH)
        return carry

    lax.fori_loop(0, turns, turn, 0)


def drag(current, speed):
    gap = current - speed
    return DRAG_COEF * jnp.sqrt(gap * gap + SPEED_FLOOR**2)


def statics(conc, thick, kind, un, vn, tx, ty, uo, vo):
    ice = jnp.where(kind == 2.0, 1.0, 0.0).astype(jnp.float32)
    open_water = jnp.where(kind == 1.0, 1.0, 0.0).astype(jnp.float32)
    push = ice * (thick * jnp.exp(-C_STAR * (1.0 - conc))) * (1.0 / ALPHA_EVP)
    inv_mass = 1.0 / (conc * thick)
    return (
        push,
        ice,
        inv_mass,
        un + tx * inv_mass,
        vn + ty * inv_mass,
        open_water * uo,
        open_water * vo,
    )


KEEP = 1.0 - 1.0 / ALPHA_EVP


def stress_rule(s1, s2, s12, div, ten, shear4, div4, ten4, shear, push, ice):
    delta = jnp.sqrt(div * div + 0.25 * (ten * ten) + (1.0 / 64.0) * (shear4 * shear4))
    rate = push / (delta + DELTA_MIN)
    delta_k = jnp.sqrt(
        (1.0 / 16.0) * (div4 * div4 + 0.25 * (ten4 * ten4)) + 0.25 * (shear * shear)
    )
    rate_k = push / (delta_k + DELTA_MIN)
    keep = KEEP * ice
    return (
        keep * s1 + rate * (div - delta),
        keep * s2 + rate * (0.25 * ten),
        keep * s12 + rate_k * (0.125 * shear),
    )


def vel_rule(now, start, force, cur, inv_mass, turn, ice, water):
    w = drag(cur, now)
    top = BETA_EVP * now + start + (force + w * cur) * inv_mass + turn
    return ice * (top / (BETA_EVP + 1.0 + w * inv_mass)) + water


def kernel(
    n_gx, n_gy, forcing, ice_state, velocity, stress, kinds,
    out_vel, out_stress, out_ocean,
    nat_f, nat_i, nat_v, nat_s, nat_k, res_v, res_s, res_o,
    V, S, X, ST, UP, DN, SDN, NUP, cor,
    tile, MP, MV, MS, MST, MN, G, GN,
    in_sem, out_sem, send_sem, recv_sem, msend_sem, mrecv_sem,
):
    count = n_gx * n_gy
    me = lax.axis_index("gx") * n_gy + lax.axis_index("gy")
    cols = kinds.shape[0] * SUB
    rows = V.shape[3]
    total_rows = rows * LANES
    flip_base = cols + SUB - 1
    mrows = cols + 2 * SUB

    def device(q):
        return (q // n_gy, q % n_gy)

    left = (me + count - 1) % count
    right = (me + 1) % count
    mirror = count - 1 - me
    mir_l = (2 * count - 2 - me) % count
    mir_r = (count - me) % count

    loads = [
        pltpu.make_async_copy(a, b, in_sem.at[t])
        for t, (a, b) in enumerate(
            ((velocity, nat_v), (kinds, nat_k), (stress, nat_s), (ice_state, nat_i), (forcing, nat_f))
        )
    ]
    for c in loads:
        c.start()

    barrier = pltpu.get_barrier_semaphore()
    for q in (left, right, mirror):
        pl.semaphore_signal(barrier, inc=1, device_id=device(q), device_id_type=MESH)

    @pl.when(mir_l != me)
    def _():
        pl.semaphore_signal(barrier, inc=1, device_id=device(mir_l), device_id_type=MESH)

    @pl.when(mir_r != me)
    def _():
        pl.semaphore_signal(barrier, inc=1, device_id=device(mir_r), device_id_type=MESH)

    row_i = lax.broadcasted_iota(jnp.int32, (rows, LANES), 0)
    lane_i = lax.broadcasted_iota(jnp.int32, (rows, LANES), 1)
    lat = math.pi * (((row_i * LANES + lane_i).astype(jnp.float32) + 0.5) / total_rows - 0.5)
    cor[...] = CORIOLIS_MAX * jnp.sin(lat)

    for c in loads:
        c.wait()

    lane_t = lax.broadcasted_iota(jnp.int32, (SUB, LANES), 1)
    fields = (
        [(nat_v, f) for f in range(2)]
        + [(nat_s, f) for f in range(3)]
        + [(nat_f, f) for f in range(4)]
        + [(nat_i, f) for f in range(2)]
        + [(nat_k, None)]
    )
    last = (rows - 1) * SUB
    for b in range(cols // SUB):
        packed = jnp.zeros((SUB, LANES), jnp.float32)
        for f, (ref, g) in enumerate(fields):
            part = ref[b, last : last + SUB, :] if g is None else ref[g, b, last : last + SUB, :]
            part = part.astype(jnp.float32)
            part = pltpu.roll(part, (SUB * f + SUB) % LANES, 1)
            packed = jnp.where((lane_t >= SUB * f) & (lane_t < SUB * f + SUB), part, packed)
        tile[b * SUB : b * SUB + SUB, :] = packed

    for b in range(cols // SUB):

        def spread(r, carry):
            w = OFF + b * SUB + r
            at = pl.ds(r, rows, stride=SUB)
            for f in range(2):
                V[0, f, w] = nat_v[f, b, at, :]
            for f in range(3):
                S[0, f, w] = nat_s[f, b, at, :]
            for f in range(4):
                X[f, w] = nat_f[f, b, at, :]
            for f in range(2):
                X[4 + f, w] = nat_i[f, b, at, :]
            X[6, w] = nat_k[b, at, :].astype(jnp.float32)
            return carry

        lax.fori_loop(0, SUB, spread, 0)

    own_l, own_r = OFF, OFF + cols

    pl.semaphore_wait(
        barrier, 5 - jnp.where(mir_l == me, 1, 0) - jnp.where(mir_r == me, 1, 0)
    )

    def remote(src, dst, ssem, rsem, q):
        return pltpu.make_async_remote_copy(
            src_ref=src, dst_ref=dst, send_sem=ssem, recv_sem=rsem,
            device_id=device(q), device_id_type=MESH,
        )

    to_mirror = remote(
        tile, MP.at[pl.ds(SUB, cols)], msend_sem.at[0], mrecv_sem.at[0], mirror
    )
    to_ml = remote(
        tile.at[pl.ds(cols - SUB, SUB)], MP.at[pl.ds(0, SUB)], msend_sem.at[1], mrecv_sem.at[1], mir_l
    )
    to_mr = remote(
        tile.at[pl.ds(0, SUB)], MP.at[pl.ds(SUB + cols, SUB)], msend_sem.at[2], mrecv_sem.at[2], mir_r
    )
    to_mirror.start()

    @pl.when(mir_l != me)
    def _():
        to_ml.start()

    @pl.when(mir_r != me)
    def _():
        to_mr.start()

    sends = []
    for t, (buf, halo) in enumerate(((V.at[0], VEL_HALO), (S.at[0], REST_HALO), (X, REST_HALO))):
        sends.append(
            remote(
                buf.at[:, pl.ds(own_l, halo)], buf.at[:, pl.ds(own_r, halo)],
                send_sem.at[2 * t], recv_sem.at[2 * t], left,
            )
        )
        sends.append(
            remote(
                buf.at[:, pl.ds(own_r - halo, halo)], buf.at[:, pl.ds(own_l - halo, halo)],
                send_sem.at[2 * t + 1], recv_sem.at[2 * t + 1], right,
            )
        )
    for c in sends:
        c.start()

    def prepare(c):
        w = pl.ds(c + OFF, CH)
        got = statics(
            X[4, w], X[5, w], X[6, w], V[0, 0, w], V[0, 1, w], X[2, w], X[3, w], X[0, w], X[1, w]
        )
        for f, value in enumerate(got):
            ST[f, w] = value

    loop(0, cols, prepare)

    lane_e = lax.broadcasted_iota(jnp.int32, (rows, LANES), 1)
    row_e = lax.broadcasted_iota(jnp.int32, (rows, LANES), 0)
    at_last = lane_e == LANES - 1
    at_first = lane_e == 0
    at_top = at_last & (row_e == rows - 1)
    at_bottom = at_first & (row_e == 0)

    def shift_up(x, ghost):
        r = pltpu.roll(x, LANES - 1, 1)
        q = pltpu.roll(r, rows - 1, 0)
        return jnp.where(at_top, ghost, jnp.where(at_last, q, r))

    def shift_down(x):
        r = pltpu.roll(x, 1, 1)
        q = pltpu.roll(r, 1, 0)
        return jnp.where(at_bottom, 0.0, jnp.where(at_first, q, r))

    def put_shifts(k, c, j, u, v):
        w = c + OFF + j
        slot = pl.ds(flip_base - c - j, 1)
        UP[k, 0, w] = shift_up(u, -MV[k, 0, slot, :])
        UP[k, 1, w] = shift_up(v, -MV[k, 1, slot, :])
        DN[k, 0, w] = shift_down(u)
        DN[k, 1, w] = shift_down(v)
        G[k, 0, slot, :] = u[rows - 1 : rows, :]
        G[k, 1, slot, :] = v[rows - 1 : rows, :]

    def shift_start(c):
        for j in range(CH):
            put_shifts(0, c, j, V[0, 0, c + OFF + j], V[0, 1, c + OFF + j])

    def stress_step(k, c):
        wide = pl.ds(c + OFF - 1, CH + 2)
        w = pl.ds(c + OFF, CH)
        u, v = V[k, 0, wide], V[k, 1, wide]
        up, vp = UP[k, 0, wide], UP[k, 1, wide]
        um, vm = DN[k, 0, wide], DN[k, 1, wide]
        du = u[1:] - u[:-1]
        dup = up[1:] - up[:-1]
        dv = v[1:] - vm[1:]
        dvp = vp[1:] - v[1:]
        div = du + dv
        ten = du - dv
        dsum = div + (dup + dvp)
        tsum = ten + (dup - dvp)
        shear = (up[:-1] - u[:-1]) + (v[1:] - v[:-1])
        ssum = shear + ((u[:-1] - um[:-1]) + (vm[1:] - vm[:-1]))
        s1, s2, s12 = stress_rule(
            S[k, 0, w], S[k, 1, w], S[k, 2, w],
            div[:-1], ten[:-1], ssum[1:] + ssum[:-1],
            dsum[1:] + dsum[:-1], tsum[1:] + tsum[:-1], shear[1:],
            ST[0, w], ST[1, w],
        )
        S[k + 1, 0, w] = s1
        S[k + 1, 1, w] = s2
        S[k + 1, 2, w] = s12
        n22 = s1 - s2
        for j in range(CH):
            slot = pl.ds(flip_base - c - j, 1)
            SDN[k, c + OFF + j] = shift_down(s12[j])
            NUP[k, c + OFF + j] = shift_up(n22[j], MN[slot, :])
            GN[k, slot, :] = n22[j, rows - 1 : rows, :]

    def vel_step(k, c):
        w = pl.ds(c + OFF, CH)
        nxt = pl.ds(c + OFF, CH + 1)
        prv = pl.ds(c + OFF - 1, CH + 1)
        sr1, sr2 = S[k + 1, 0, nxt], S[k + 1, 1, nxt]
        s12 = S[k + 1, 2, prv]
        n11 = sr1 + sr2
        n22 = sr1[:-1] - sr2[:-1]
        fu = 0.5 * (n11[1:] - n11[:-1]) + (s12[1:] - SDN[k, w])
        fv = 0.5 * (NUP[k, w] - n22) + (s12[1:] - s12[:-1])
        v = V[k, 1, nxt]
        u = V[k, 0, prv]
        va = v + DN[k, 1, nxt]
        ua = u + UP[k, 0, prv]
        f = 0.25 * cor[...][None]
        ice, inv_mass = ST[1, w], ST[2, w]
        uo, vo = X[0, w], X[1, w]
        un = vel_rule(u[1:], ST[3, w], fu, uo, inv_mass, f * (va[1:] + va[:-1]), ice, ST[5, w])
        vn = vel_rule(v[:-1], ST[4, w], fv, vo, inv_mass, -f * (ua[1:] + ua[:-1]), ice, ST[6, w])
        if k + 1 < ITERS:
            V[k + 1, 0, w] = un
            V[k + 1, 1, w] = vn
            for j in range(CH):
                put_shifts(k + 1, c, j, un[j], vn[j])
            return
        ou = drag(uo, un) * (un - uo)
        ov = drag(vo, vn) * (vn - vo)
        for j in range(CH):
            b, r = c // SUB, c % SUB + j
            at = pl.ds(r, rows, stride=SUB)
            res_v[0, b, at, :] = un[j]
            res_v[1, b, at, :] = vn[j]
            res_s[0, b, at, :] = sr1[j]
            res_s[1, b, at, :] = sr2[j]
            res_s[2, b, at, :] = s12[j + 1]
            res_o[0, b, at, :] = ou[j]
            res_o[1, b, at, :] = ov[j]

    lane_m = lax.broadcasted_iota(jnp.int32, (mrows, LANES), 1)
    m_last = lane_m == LANES - 1

    def m_west(x):
        return pltpu.roll(x, 1, 0)

    def m_east(x):
        return pltpu.roll(x, mrows - 1, 0)

    def m_down(x):
        return pltpu.roll(x, 1, 1)

    def m_up(x, ghost):
        return jnp.where(m_last, ghost, pltpu.roll(x, LANES - 1, 1))

    def m_prepare():
        whole = MP[...]
        raw = [
            whole if (LANES - SUB - SUB * f) % LANES == 0
            else pltpu.roll(whole, (LANES - SUB - SUB * f) % LANES, 1)
            for f in range(12)
        ]
        u, v, s1, s2, s12, uo, vo, tx, ty, conc, thick, kind = raw
        MV[0, 0], MV[0, 1] = u, v
        MS[0], MS[1], MS[2] = s1, s2, s12
        for f, value in enumerate(statics(conc, thick, kind, u, v, tx, ty, uo, vo)):
            MST[f] = value
        MST[7] = uo
        MST[8] = vo

    def m_stress(k):
        u, v = MV[k, 0], MV[k, 1]
        up, vp = m_up(u, -G[k, 0]), m_up(v, -G[k, 1])
        um, vm = m_down(u), m_down(v)
        du = u - m_west(u)
        dup = up - m_west(up)
        dv = v - vm
        dvp = vp - v
        div, ten = du + dv, du - dv
        dsum, tsum = div + (dup + dvp), ten + (dup - dvp)
        shear = (up - u) + (m_east(v) - v)
        ssum = shear + ((u - um) + (m_east(vm) - vm))
        src = 3 * k
        got = stress_rule(
            MS[src], MS[src + 1], MS[src + 2], div, ten, ssum + m_west(ssum),
            dsum + m_east(dsum), tsum + m_east(tsum), shear, MST[0], MST[1],
        )
        for f in range(3):
            MS[src + 3 + f] = got[f]
        MN[...] = got[0] - got[1]

    def m_vel(k):
        src = 3 * k + 3
        s1, s2, s12 = MS[src], MS[src + 1], MS[src + 2]
        n11, n22 = s1 + s2, s1 - s2
        u, v = MV[k, 0], MV[k, 1]
        up, vm = m_up(u, -G[k, 0]), m_down(v)
        fu = 0.5 * (m_east(n11) - n11) + (s12 - m_down(s12))
        fv = 0.5 * (m_up(n22, GN[k]) - n22) + (s12 - m_west(s12))
        va, ua = v + vm, u + up
        f = 0.25 * cor[rows - 1 : rows, :]
        MV[k + 1, 0] = vel_rule(
            u, MST[3], fu, MST[7], MST[2], f * (va + m_east(va)), MST[1], MST[5]
        )
        MV[k + 1, 1] = vel_rule(
            v, MST[4], fv, MST[8], MST[2], -f * (ua + m_west(ua)), MST[1], MST[6]
        )

    to_mirror.wait_recv()

    @pl.when(mir_l != me)
    def _():
        to_ml.wait_recv()

    @pl.when(mir_l == me)
    def _():
        MP[0:SUB, :] = tile[cols - SUB : cols, :]

    @pl.when(mir_r != me)
    def _():
        to_mr.wait_recv()

    @pl.when(mir_r == me)
    def _():
        MP[SUB + cols : mrows, :] = tile[0:SUB, :]

    m_prepare()

    def sweep(start_parts, stress_parts, vel_parts):
        for lo, hi in start_parts:
            loop(lo, hi, shift_start)
        for k in range(len(stress_parts)):
            m_stress(k)
            for lo, hi in stress_parts[k]:
                loop(lo, hi, functools.partial(stress_step, k))
            if k + 1 < ITERS:
                m_vel(k)
                for lo, hi in vel_parts[k]:
                    loop(lo, hi, functools.partial(vel_step, k))

    inner = (1, 4, 6)
    inner_vel = (3, 5, 8)
    sweep(
        [(0, cols)],
        [[(a, cols - a)] for a in inner],
        [[(a, cols - a)] for a in inner_vel],
    )

    for c in sends:
        c.wait_recv()

    loop(-VEL_HALO, 0, shift_start)
    loop(cols, cols + VEL_HALO, shift_start)
    edge = REST_HALO + 1
    loop(-edge, 0, prepare)
    loop(cols, cols + edge, prepare)

    def both(reach, a):
        return [(-reach, a), (cols - a, cols + reach)]

    sweep(
        [],
        [both(r, a) for r, a in zip(STRESS_REACH[:3], inner)]
        + [[(-STRESS_REACH[3], cols + STRESS_REACH[3])]],
        [both(r, a) for r, a in zip(VEL_REACH[:2], inner_vel)]
        + [[(-VEL_REACH[2], cols + VEL_REACH[2])]],
    )

    outs = []
    for b in range(cols // SUB):
        for c in range(b * SUB, (b + 1) * SUB, CH):
            vel_step(ITERS - 1, c)
        for t, (src, dst) in enumerate(((res_v, out_vel), (res_s, out_stress), (res_o, out_ocean))):
            outs.append(
                pltpu.make_async_copy(src.at[:, b], dst.at[:, b], out_sem.at[3 * b + t])
            )
            outs[-1].start()

    to_mirror.wait_send()

    @pl.when(mir_l != me)
    def _():
        to_ml.wait_send()

    @pl.when(mir_r != me)
    def _():
        to_mr.wait_send()

    for c in sends:
        c.wait_send()
    for c in outs:
        c.wait()


def to_tiles(x):
    lead, (c, r) = x.shape[:-2], x.shape[-2:]
    x = x.reshape(lead + (c // SUB, SUB, r // LANES, LANES))
    return jnp.swapaxes(x, -3, -2).reshape(lead + (c // SUB, r // LANES * SUB, LANES))


def from_tiles(x, c, r):
    lead = x.shape[:-3]
    x = x.reshape(lead + (c // SUB, r // LANES, SUB, LANES))
    return jnp.swapaxes(x, -3, -2).reshape(lead + (c, r))


def on_device(n_gx, n_gy, forcing, ice_state, velocity, stress, ice_mask):
    cols, height = ice_mask.shape
    rows = height // LANES
    blocks = cols // SUB
    width = cols + 2 * OFF
    f32 = jnp.float32

    def tiles(n):
        return (n, blocks, rows * SUB, LANES)

    def vmem(*shape):
        return pltpu.VMEM(shape, f32)

    mrows = cols + 2 * SUB
    dma = pltpu.SemaphoreType.DMA
    scratch = [
        vmem(*tiles(4)), vmem(*tiles(2)), vmem(*tiles(2)), vmem(*tiles(3)),
        pltpu.VMEM(tiles(1)[1:], jnp.int32),
        vmem(*tiles(2)), vmem(*tiles(3)), vmem(*tiles(2)),
        vmem(ITERS, 2, width, rows, LANES),
        vmem(ITERS + 1, 3, width, rows, LANES),
        vmem(7, width, rows, LANES),
        vmem(7, width, rows, LANES),
        vmem(ITERS, 2, width, rows, LANES),
        vmem(ITERS, 2, width, rows, LANES),
        vmem(ITERS, width, rows, LANES),
        vmem(ITERS, width, rows, LANES),
        vmem(rows, LANES),
        vmem(cols, LANES),
        vmem(mrows, LANES),
        vmem(ITERS, 2, mrows, LANES),
        vmem(3 * (ITERS + 1), mrows, LANES),
        vmem(9, mrows, LANES),
        vmem(mrows, LANES),
        vmem(ITERS, 2, mrows, LANES),
        vmem(ITERS, mrows, LANES),
        dma((5,)), dma((3 * blocks,)), dma((6,)), dma((6,)), dma((3,)), dma((3,)),
    ]
    any_spec = pl.BlockSpec(memory_space=pl.ANY)
    vel, str_, ocean = pl.pallas_call(
        functools.partial(kernel, n_gx, n_gy),
        out_shape=[jax.ShapeDtypeStruct(tiles(n), f32) for n in (2, 3, 2)],
        in_specs=[any_spec] * 5,
        out_specs=[any_spec] * 3,
        scratch_shapes=scratch,
        compiler_params=pltpu.CompilerParams(
            collective_id=0, has_side_effects=True, vmem_limit_bytes=60 * 1024 * 1024
        ),
    )(to_tiles(forcing), to_tiles(ice_state), to_tiles(velocity), to_tiles(stress), to_tiles(ice_mask))
    return (
        from_tiles(vel, cols, height),
        from_tiles(str_, cols, height),
        from_tiles(ocean, cols, height),
    )


def solution(mesh):
    spec = P(None, ("gx", "gy"), None)
    return jax.shard_map(
        functools.partial(on_device, mesh.shape["gx"], mesh.shape["gy"]),
        mesh=mesh,
        in_specs=(spec, spec, spec, spec, P(("gx", "gy"), None)),
        out_specs=(spec, spec, spec),
        check_vma=False,
    )
```

profile of v0, /device:TPU:1, one launch (start us, length us, event | category | flops | bytes accessed | tf_op | source)
XLA Modules:
  0.0 33.1 jit_solution(1073456826638007968)
XLA Ops:
  0.6 28.9 %shard_map.76 = (f32[2,2,128,128]{3,2,1,0:T(8,128)}, f32[3,2,128,128]{3,2,1,0:T(8,128)}, f32[2,2,128,128]{3,2,1,0:T(8,128)}) custom-call(f32[4,2,128,128]{3,2,1,0:T(8,128)} %bitcast.40, f32[2,2,128,128]{3,2,1,0:T(8,128)} %bitcast.45, f32[2,2,128,128]{3,2,1,0:T(8,128)} %bitcast.46, f32[3,2,128,128]{3,2,1,0:T(8,128)} %bitcast.42, s32[2,128,128]{2,1,0:T(8,128)} %bitcast.47), custom_call_target="tpu_custom_call" | custom-call | tf_op jit(solution)/shard_map/pallas_call | solution.py:540
  29.6 0.0 copy-start
  29.6 1.7 %copy.11 = f32[2,16,2048]{2,1,0:T(8,128)} copy(f32[2,16,2048]{2,1,0:T(8,128)} %bitcast.44) | data formatting | bytes 524288
  31.3 0.0 copy-done
  31.3 0.0 copy-start.1
  31.3 0.7 %copy.12 = f32[3,16,2048]{2,1,0:T(8,128)} copy(f32[3,16,2048]{2,1,0:T(8,128)S(1)} %bitcast.41) | data formatting | bytes 786432
  32.1 0.3 %copy-done.1 = f32[2,2,128,128]{3,2,1,0:T(8,128)S(1)} copy-done((f32[2,2,128,128]{3,2,1,0:T(8,128)S(1)}, f32[2,2,128,128]{3,2,1,0:T(8,128)}, u32[]{:S(2)}) %copy-start.1) | copy-done | bytes 262168
  32.4 0.7 %copy.13 = f32[2,16,2048]{2,1,0:T(8,128)} copy(f32[2,16,2048]{2,1,0:T(8,128)S(1)} %bitcast.43) | data formatting | bytes 524288
Async XLA Ops:
  29.6 1.7 %copy-start = (f32[3,2,128,128]{3,2,1,0:T(8,128)S(1)}, f32[3,2,128,128]{3,2,1,0:T(8,128)}, u32[]{:S(2)}) copy-start(f32[3,2,128,128]{3,2,1,0:T(8,128)} %get-tuple-element.7) | copy-start | bytes 1179652
  31.3 1.1 %copy-start.1 = (f32[2,2,128,128]{3,2,1,0:T(8,128)S(1)}, f32[2,2,128,128]{3,2,1,0:T(8,128)}, u32[]{:S(2)}) copy-start(f32[2,2,128,128]{3,2,1,0:T(8,128)} %get-tuple-element.8) | copy-start | bytes 786436
where the time goes:
time: 33.3 us; the launch traced here: 33.1 us
  Pallas kernels  28.9 us (87%)
  local copies, waits for them, and re-layouts  3.52 us (11%)
  between operations  0.65 us (2%)
    pallas_call x1, Pallas kernels, on_device(): pl.pallas_call(functools.partial(kernel, n_gx, n_gy), out_shape=[jax.Shap...  28.9 us
    unnamed x7, local copies, waits for them, and re-layouts  3.52 us

commit v1 on v0

--- a/solution.py
+++ b/solution.py
@@ -29,10 +29,15 @@
 
 
 def loop(lo, hi, body):
-    turns = (hi - lo) // CH
-
+    half = (hi - lo) // (2 * CH)
+    pairs(lo, hi - half * CH, half, body)
+    if (hi - lo) // CH > 2 * half:
+        body([lo + half * CH])
+
+
+def pairs(lo, other, turns, body):
     def turn(t, carry):
-        body(lo + t * CH)
+        body([lo + t * CH, other + t * CH])
         return carry
 
     lax.fori_loop(0, turns, turn, 0)
@@ -84,16 +89,15 @@
 
 
 def kernel(
-    n_gx, n_gy, forcing, ice_state, velocity, stress, kinds,
-    out_vel, out_stress, out_ocean,
-    nat_f, nat_i, nat_v, nat_s, nat_k, res_v, res_s, res_o,
+    n_gx, n_gy, nat_f, nat_i, nat_v, nat_s, nat_k,
+    res_v, res_s, res_o,
     V, S, X, ST, UP, DN, SDN, NUP, cor,
     tile, MP, MV, MS, MST, MN, G, GN,
-    in_sem, out_sem, send_sem, recv_sem, msend_sem, mrecv_sem,
+    send_sem, recv_sem, msend_sem, mrecv_sem,
 ):
     count = n_gx * n_gy
     me = lax.axis_index("gx") * n_gy + lax.axis_index("gy")
-    cols = kinds.shape[0] * SUB
+    cols = nat_k.shape[0] * SUB
     rows = V.shape[3]
     total_rows = rows * LANES
     flip_base = cols + SUB - 1
@@ -108,15 +112,6 @@
     mir_l = (2 * count - 2 - me) % count
     mir_r = (count - me) % count
 
-    loads = [
-        pltpu.make_async_copy(a, b, in_sem.at[t])
-        for t, (a, b) in enumerate(
-            ((velocity, nat_v), (kinds, nat_k), (stress, nat_s), (ice_state, nat_i), (forcing, nat_f))
-        )
-    ]
-    for c in loads:
-        c.start()
-
     barrier = pltpu.get_barrier_semaphore()
     for q in (left, right, mirror):
         pl.semaphore_signal(barrier, inc=1, device_id=device(q), device_id_type=MESH)
@@ -133,9 +128,6 @@
     lane_i = lax.broadcasted_iota(jnp.int32, (rows, LANES), 1)
     lat = math.pi * (((row_i * LANES + lane_i).astype(jnp.float32) + 0.5) / total_rows - 0.5)
     cor[...] = CORIOLIS_MAX * jnp.sin(lat)
-
-    for c in loads:
-        c.wait()
 
     lane_t = lax.broadcasted_iota(jnp.int32, (SUB, LANES), 1)
     fields = (
@@ -221,7 +213,11 @@
     for c in sends:
         c.start()
 
-    def prepare(c):
+    def prepare(cs):
+        for c in cs:
+            prepare_pair(c)
+
+    def prepare_pair(c):
         w = pl.ds(c + OFF, CH)
         got = statics(
             X[4, w], X[5, w], X[6, w], V[0, 0, w], V[0, 1, w], X[2, w], X[3, w], X[0, w], X[1, w]
@@ -258,11 +254,19 @@
         G[k, 0, slot, :] = u[rows - 1 : rows, :]
         G[k, 1, slot, :] = v[rows - 1 : rows, :]
 
-    def shift_start(c):
-        for j in range(CH):
-            put_shifts(0, c, j, V[0, 0, c + OFF + j], V[0, 1, c + OFF + j])
-
-    def stress_step(k, c):
+    def shift_start(cs):
+        got = [
+            (c, j, V[0, 0, c + OFF + j], V[0, 1, c + OFF + j]) for c in cs for j in range(CH)
+        ]
+        for c, j, u, v in got:
+            put_shifts(0, c, j, u, v)
+
+    def stress_step(k, cs):
+        got = [stress_of(k, c) for c in cs]
+        for c, (s1, s2, s12) in zip(cs, got):
+            put_stress(k, c, s1, s2, s12)
+
+    def stress_of(k, c):
         wide = pl.ds(c + OFF - 1, CH + 2)
         w = pl.ds(c + OFF, CH)
         u, v = V[k, 0, wide], V[k, 1, wide]
@@ -278,23 +282,36 @@
         tsum = ten + (dup - dvp)
         shear = (up[:-1] - u[:-1]) + (v[1:] - v[:-1])
         ssum = shear + ((u[:-1] - um[:-1]) + (vm[1:] - vm[:-1]))
-        s1, s2, s12 = stress_rule(
+        return stress_rule(
             S[k, 0, w], S[k, 1, w], S[k, 2, w],
             div[:-1], ten[:-1], ssum[1:] + ssum[:-1],
             dsum[1:] + dsum[:-1], tsum[1:] + tsum[:-1], shear[1:],
             ST[0, w], ST[1, w],
         )
+
+    def put_stress(k, c, s1, s2, s12):
+        w = pl.ds(c + OFF, CH)
+        ups, downs = [], []
+        n22 = s1 - s2
+        for j in range(CH):
+            slot = pl.ds(flip_base - c - j, 1)
+            downs.append(shift_down(s12[j]))
+            ups.append(shift_up(n22[j], MN[slot, :]))
         S[k + 1, 0, w] = s1
         S[k + 1, 1, w] = s2
         S[k + 1, 2, w] = s12
-        n22 = s1 - s2
         for j in range(CH):
             slot = pl.ds(flip_base - c - j, 1)
-            SDN[k, c + OFF + j] = shift_down(s12[j])
-            NUP[k, c + OFF + j] = shift_up(n22[j], MN[slot, :])
+            SDN[k, c + OFF + j] = downs[j]
+            NUP[k, c + OFF + j] = ups[j]
             GN[k, slot, :] = n22[j, rows - 1 : rows, :]
 
-    def vel_step(k, c):
+    def vel_step(k, cs):
+        got = [vel_of(k, c) for c in cs]
+        for c, values in zip(cs, got):
+            put_vel(k, c, *values)
+
+    def vel_of(k, c):
         w = pl.ds(c + OFF, CH)
         nxt = pl.ds(c + OFF, CH + 1)
         prv = pl.ds(c + OFF - 1, CH + 1)
@@ -313,6 +330,10 @@
         uo, vo = X[0, w], X[1, w]
         un = vel_rule(u[1:], ST[3, w], fu, uo, inv_mass, f * (va[1:] + va[:-1]), ice, ST[5, w])
         vn = vel_rule(v[:-1], ST[4, w], fv, vo, inv_mass, -f * (ua[1:] + ua[:-1]), ice, ST[6, w])
+        return un, vn, uo, vo, sr1, sr2, s12
+
+    def put_vel(k, c, un, vn, uo, vo, sr1, sr2, s12):
+        w = pl.ds(c + OFF, CH)
         if k + 1 < ITERS:
             V[k + 1, 0, w] = un
             V[k + 1, 1, w] = vn
@@ -420,17 +441,23 @@
 
     m_prepare()
 
+    def run(part, body):
+        if len(part) == 3:
+            pairs(*part, body)
+        else:
+            loop(*part, body)
+
     def sweep(start_parts, stress_parts, vel_parts):
         for lo, hi in start_parts:
             loop(lo, hi, shift_start)
         for k in range(len(stress_parts)):
             m_stress(k)
-            for lo, hi in stress_parts[k]:
-                loop(lo, hi, functools.partial(stress_step, k))
+            for part in stress_parts[k]:
+                run(part, functools.partial(stress_step, k))
             if k + 1 < ITERS:
                 m_vel(k)
-                for lo, hi in vel_parts[k]:
-                    loop(lo, hi, functools.partial(vel_step, k))
+                for part in vel_parts[k]:
+                    run(part, functools.partial(vel_step, k))
 
     inner = (1, 4, 6)
     inner_vel = (3, 5, 8)
@@ -443,14 +470,12 @@
     for c in sends:
         c.wait_recv()
 
-    loop(-VEL_HALO, 0, shift_start)
-    loop(cols, cols + VEL_HALO, shift_start)
+    pairs(-VEL_HALO, cols, VEL_HALO // CH, shift_start)
     edge = REST_HALO + 1
-    loop(-edge, 0, prepare)
-    loop(cols, cols + edge, prepare)
+    pairs(-edge, cols, edge // CH, prepare)
 
     def both(reach, a):
-        return [(-reach, a), (cols - a, cols + reach)]
+        return [(-reach, cols - a, (reach + a) // CH)]
 
     sweep(
         [],
@@ -460,15 +485,8 @@
         + [[(-VEL_REACH[2], cols + VEL_REACH[2])]],
     )
 
-    outs = []
-    for b in range(cols // SUB):
-        for c in range(b * SUB, (b + 1) * SUB, CH):
-            vel_step(ITERS - 1, c)
-        for t, (src, dst) in enumerate(((res_v, out_vel), (res_s, out_stress), (res_o, out_ocean))):
-            outs.append(
-                pltpu.make_async_copy(src.at[:, b], dst.at[:, b], out_sem.at[3 * b + t])
-            )
-            outs[-1].start()
+    for c in range(0, cols, 2 * CH):
+        vel_step(ITERS - 1, [c, c + CH])
 
     to_mirror.wait_send()
 
@@ -482,8 +500,16 @@
 
     for c in sends:
         c.wait_send()
-    for c in outs:
-        c.wait()
+
+def write_out(a, b, c, out_a, out_b, out_c, sem):
+    copies = [
+        pltpu.make_async_copy(src, dst, sem.at[t])
+        for t, (src, dst) in enumerate(((b, out_b), (a, out_a), (c, out_c)))
+    ]
+    for copy in copies:
+        copy.start()
+    for copy in copies:
+        copy.wait()
 
 
 def to_tiles(x):
@@ -514,9 +540,6 @@
     mrows = cols + 2 * SUB
     dma = pltpu.SemaphoreType.DMA
     scratch = [
-        vmem(*tiles(4)), vmem(*tiles(2)), vmem(*tiles(2)), vmem(*tiles(3)),
-        pltpu.VMEM(tiles(1)[1:], jnp.int32),
-        vmem(*tiles(2)), vmem(*tiles(3)), vmem(*tiles(2)),
         vmem(ITERS, 2, width, rows, LANES),
         vmem(ITERS + 1, 3, width, rows, LANES),
         vmem(7, width, rows, LANES),
@@ -534,19 +557,29 @@
         vmem(mrows, LANES),
         vmem(ITERS, 2, mrows, LANES),
         vmem(ITERS, mrows, LANES),
-        dma((5,)), dma((3 * blocks,)), dma((6,)), dma((6,)), dma((3,)), dma((3,)),
+        dma((6,)), dma((6,)), dma((3,)), dma((3,)),
     ]
-    any_spec = pl.BlockSpec(memory_space=pl.ANY)
-    vel, str_, ocean = pl.pallas_call(
+    any_spec = pl.BlockSpec(memory_space=pltpu.HBM)
+    vmem_spec = pl.BlockSpec(memory_space=pltpu.VMEM)
+    shapes = [jax.ShapeDtypeStruct(tiles(n), f32) for n in (2, 3, 2)]
+    results = pl.pallas_call(
         functools.partial(kernel, n_gx, n_gy),
-        out_shape=[jax.ShapeDtypeStruct(tiles(n), f32) for n in (2, 3, 2)],
-        in_specs=[any_spec] * 5,
-        out_specs=[any_spec] * 3,
+        out_shape=shapes,
+        in_specs=[vmem_spec] * 5,
+        out_specs=[vmem_spec] * 3,
         scratch_shapes=scratch,
         compiler_params=pltpu.CompilerParams(
-            collective_id=0, has_side_effects=True, vmem_limit_bytes=60 * 1024 * 1024
+            collective_id=0, has_side_effects=True, vmem_limit_bytes=44 * 1024 * 1024
         ),
     )(to_tiles(forcing), to_tiles(ice_state), to_tiles(velocity), to_tiles(stress), to_tiles(ice_mask))
+    vel, str_, ocean = pl.pallas_call(
+        write_out,
+        out_shape=shapes,
+        in_specs=[vmem_spec] * 3,
+        out_specs=[any_spec] * 3,
+        scratch_shapes=[dma((3,))],
+        compiler_params=pltpu.CompilerParams(vmem_limit_bytes=8 * 1024 * 1024),
+    )(*results)
     return (
         from_tiles(vel, cols, height),
         from_tiles(str_, cols, height),

time: 33.3 us -> 32 us (0.961)
  Pallas kernels: 28.9 us -> 26.2 us
  local copies, waits for them, and re-layouts: 3.52 us -> 4.83 us
    pallas_call x1 -> x2, Pallas kernels: 28.9 us -> 26.2 us  [the longest x1 25.2 us: on_device(): pl.pallas_call(functools.partial(kernel, n_gx, n_gy), out_shape=shapes, i...]
    unnamed x7 -> x10, local copies, waits for them, and re-layouts: 3.52 us -> 4.83 us
where the time goes in v1:
time: 32 us; the launch traced here: 31.7 us
  Pallas kernels  26.2 us (82%)
  local copies, waits for them, and re-layouts  4.83 us (15%)
  between operations  0.65 us (2%)
    pallas_call x1, Pallas kernels, on_device(): pl.pallas_call(functools.partial(kernel, n_gx, n_gy), out_shape=shapes, i...  25.2 us
    unnamed x10, local copies, waits for them, and re-layouts  4.83 us
    pallas_call x1, Pallas kernels, on_device(): pl.pallas_call(write_out, out_shape=shapes, in_specs=[vmem_spec] * 3, out...  0.95 us

profile of v1, /device:TPU:1, one launch (start us, length us, event | category | flops | bytes accessed | tf_op | source)
XLA Modules:
  0.0 31.7 jit_solution(17523161393899305749)
XLA Ops:
  0.6 0.0 copy-start
  0.6 1.0 %copy-done = f32[4,16,2048]{2,1,0:T(8,128)S(1)} copy-done((f32[4,16,2048]{2,1,0:T(8,128)S(1)}, f32[4,16,2048]{2,1,0:T(8,128)}, u32[]{:S(2)}) %copy-start) | copy-done | bytes 524312
  1.7 0.0 copy-start.1
  1.7 1.0 %copy-done.1 = f32[3,16,2048]{2,1,0:T(8,128)S(1)} copy-done((f32[3,16,2048]{2,1,0:T(8,128)S(1)}, f32[3,16,2048]{2,1,0:T(8,128)}, u32[]{:S(2)}) %copy-start.1) | copy-done | bytes 393240
  2.7 0.0 copy-start.2
  2.7 0.9 %copy-done.2 = f32[2,16,2048]{2,1,0:T(8,128)S(1)} copy-done((f32[2,16,2048]{2,1,0:T(8,128)S(1)}, f32[2,16,2048]{2,1,0:T(8,128)}, u32[]{:S(2)}) %copy-start.2) | copy-done | bytes 262168
  3.6 0.0 copy-start.3
  3.6 0.9 %copy-done.3 = f32[2,16,2048]{2,1,0:T(8,128)S(1)} copy-done((f32[2,16,2048]{2,1,0:T(8,128)S(1)}, f32[2,16,2048]{2,1,0:T(8,128)}, u32[]{:S(2)}) %copy-start.3) | copy-done | bytes 262168
  4.6 0.0 copy-start.4
  4.6 0.9 %copy-done.4 = s32[16,2048]{1,0:T(8,128)S(1)} copy-done((s32[16,2048]{1,0:T(8,128)S(1)}, s32[16,2048]{1,0:T(8,128)}, u32[]{:S(2)}) %copy-start.4) | copy-done | bytes 131096
  5.5 25.2 %shard_map.76 = (f32[2,2,128,128]{3,2,1,0:T(8,128)S(1)}, f32[3,2,128,128]{3,2,1,0:T(8,128)S(1)}, f32[2,2,128,128]{3,2,1,0:T(8,128)S(1)}) custom-call(f32[4,2,128,128]{3,2,1,0:T(8,128)S(1)} %bitcast.40, f32[2,2,128,128]{3,2,1,0:T(8,128)S(1)} %bitcast.42, f32[2,2,128,128]{3,2,1,0:T(8,128)S(1)} %bitcast.43, f32[3,2,128,128]{3,2,1,0:T(8,128)S(1)} %bitcast.41, ...), custom_call_target="tpu_custom_call" | custom-call | tf_op jit(solution)/shard_map/pallas_call | solution.py:565
  30.7 0.9 %shard_map.77 = (f32[2,2,128,128]{3,2,1,0:T(8,128)}, f32[3,2,128,128]{3,2,1,0:T(8,128)}, f32[2,2,128,128]{3,2,1,0:T(8,128)}) custom-call(f32[2,2,128,128]{3,2,1,0:T(8,128)S(1)} %get-tuple-element.9.a, f32[3,2,128,128]{3,2,1,0:T(8,128)S(1)} %get-tuple-element.10.b, f32[2,2,128,128]{3,2,1,0:T(8,128)S(1)} %get-tuple-element.11.c), custom_call_target="tpu_custom_call" | custom-call | tf_op jit(solution)/shard_map/pallas_call | solution.py:575
Async XLA Ops:
  0.6 1.0 %copy-start = (f32[4,16,2048]{2,1,0:T(8,128)S(1)}, f32[4,16,2048]{2,1,0:T(8,128)}, u32[]{:S(2)}) copy-start(f32[4,16,2048]{2,1,0:T(8,128)} %param.5) | copy-start | bytes 1572868
  1.7 1.0 %copy-start.1 = (f32[3,16,2048]{2,1,0:T(8,128)S(1)}, f32[3,16,2048]{2,1,0:T(8,128)}, u32[]{:S(2)}) copy-start(f32[3,16,2048]{2,1,0:T(8,128)} %param.8) | copy-start | bytes 1179652
  2.7 0.9 %copy-start.2 = (f32[2,16,2048]{2,1,0:T(8,128)S(1)}, f32[2,16,2048]{2,1,0:T(8,128)}, u32[]{:S(2)}) copy-start(f32[2,16,2048]{2,1,0:T(8,128)} %param.6) | copy-start | bytes 786436
  3.6 0.9 %copy-start.3 = (f32[2,16,2048]{2,1,0:T(8,128)S(1)}, f32[2,16,2048]{2,1,0:T(8,128)}, u32[]{:S(2)}) copy-start(f32[2,16,2048]{2,1,0:T(8,128)} %param.7) | copy-start | bytes 786436
  4.6 0.9 %copy-start.4 = (s32[16,2048]{1,0:T(8,128)S(1)}, s32[16,2048]{1,0:T(8,128)}, u32[]{:S(2)}) copy-start(s32[16,2048]{1,0:T(8,128)} %param.9) | copy-start | bytes 393220

commit v2 on v1

--- a/solution.py
+++ b/solution.py
@@ -89,15 +89,16 @@
 
 
 def kernel(
-    n_gx, n_gy, nat_f, nat_i, nat_v, nat_s, nat_k,
-    res_v, res_s, res_o,
+    n_gx, n_gy, forcing, ice_state, velocity, stress, kinds,
+    out_vel, out_stress, out_ocean,
+    nat_f, nat_i, nat_v, nat_s, nat_k, res_v, res_s, res_o,
     V, S, X, ST, UP, DN, SDN, NUP, cor,
     tile, MP, MV, MS, MST, MN, G, GN,
-    send_sem, recv_sem, msend_sem, mrecv_sem,
+    in_sem, out_sem, send_sem, recv_sem, msend_sem, mrecv_sem,
 ):
     count = n_gx * n_gy
     me = lax.axis_index("gx") * n_gy + lax.axis_index("gy")
-    cols = nat_k.shape[0] * SUB
+    cols = kinds.shape[0] * SUB
     rows = V.shape[3]
     total_rows = rows * LANES
     flip_base = cols + SUB - 1
@@ -112,6 +113,15 @@
     mir_l = (2 * count - 2 - me) % count
     mir_r = (count - me) % count
 
+    loads = [
+        pltpu.make_async_copy(a, b, in_sem.at[t])
+        for t, (a, b) in enumerate(
+            ((velocity, nat_v), (kinds, nat_k), (stress, nat_s), (ice_state, nat_i), (forcing, nat_f))
+        )
+    ]
+    for c in loads:
+        c.start()
+
     barrier = pltpu.get_barrier_semaphore()
     for q in (left, right, mirror):
         pl.semaphore_signal(barrier, inc=1, device_id=device(q), device_id_type=MESH)
@@ -128,6 +138,9 @@
     lane_i = lax.broadcasted_iota(jnp.int32, (rows, LANES), 1)
     lat = math.pi * (((row_i * LANES + lane_i).astype(jnp.float32) + 0.5) / total_rows - 0.5)
     cor[...] = CORIOLIS_MAX * jnp.sin(lat)
+
+    for c in loads:
+        c.wait()
 
     lane_t = lax.broadcasted_iota(jnp.int32, (SUB, LANES), 1)
     fields = (
@@ -485,8 +498,15 @@
         + [[(-VEL_REACH[2], cols + VEL_REACH[2])]],
     )
 
-    for c in range(0, cols, 2 * CH):
-        vel_step(ITERS - 1, [c, c + CH])
+    outs = []
+    for b in range(cols // SUB):
+        for c in range(b * SUB, (b + 1) * SUB, 2 * CH):
+            vel_step(ITERS - 1, [c, c + CH])
+        for t, (src, dst) in enumerate(((res_v, out_vel), (res_s, out_stress), (res_o, out_ocean))):
+            outs.append(
+                pltpu.make_async_copy(src.at[:, b], dst.at[:, b], out_sem.at[3 * b + t])
+            )
+            outs[-1].start()
 
     to_mirror.wait_send()
 
@@ -500,16 +520,8 @@
 
     for c in sends:
         c.wait_send()
-
-def write_out(a, b, c, out_a, out_b, out_c, sem):
-    copies = [
-        pltpu.make_async_copy(src, dst, sem.at[t])
-        for t, (src, dst) in enumerate(((b, out_b), (a, out_a), (c, out_c)))
-    ]
-    for copy in copies:
-        copy.start()
-    for copy in copies:
-        copy.wait()
+    for c in outs:
+        c.wait()
 
 
 def to_tiles(x):
@@ -540,6 +552,9 @@
     mrows = cols + 2 * SUB
     dma = pltpu.SemaphoreType.DMA
     scratch = [
+        vmem(*tiles(4)), vmem(*tiles(2)), vmem(*tiles(2)), vmem(*tiles(3)),
+        pltpu.VMEM(tiles(1)[1:], jnp.int32),
+        vmem(*tiles(2)), vmem(*tiles(3)), vmem(*tiles(2)),
         vmem(ITERS, 2, width, rows, LANES),
         vmem(ITERS + 1, 3, width, rows, LANES),
         vmem(7, width, rows, LANES),
@@ -557,29 +572,19 @@
         vmem(mrows, LANES),
         vmem(ITERS, 2, mrows, LANES),
         vmem(ITERS, mrows, LANES),
-        dma((6,)), dma((6,)), dma((3,)), dma((3,)),
+        dma((5,)), dma((3 * blocks,)), dma((6,)), dma((6,)), dma((3,)), dma((3,)),
     ]
-    any_spec = pl.BlockSpec(memory_space=pltpu.HBM)
-    vmem_spec = pl.BlockSpec(memory_space=pltpu.VMEM)
-    shapes = [jax.ShapeDtypeStruct(tiles(n), f32) for n in (2, 3, 2)]
-    results = pl.pallas_call(
+    any_spec = pl.BlockSpec(memory_space=pl.ANY)
+    vel, str_, ocean = pl.pallas_call(
         functools.partial(kernel, n_gx, n_gy),
-        out_shape=shapes,
-        in_specs=[vmem_spec] * 5,
-        out_specs=[vmem_spec] * 3,
+        out_shape=[jax.ShapeDtypeStruct(tiles(n), f32) for n in (2, 3, 2)],
+        in_specs=[any_spec] * 5,
+        out_specs=[any_spec] * 3,
         scratch_shapes=scratch,
         compiler_params=pltpu.CompilerParams(
-            collective_id=0, has_side_effects=True, vmem_limit_bytes=44 * 1024 * 1024
+            collective_id=0, has_side_effects=True, vmem_limit_bytes=60 * 1024 * 1024
         ),
     )(to_tiles(forcing), to_tiles(ice_state), to_tiles(velocity), to_tiles(stress), to_tiles(ice_mask))
-    vel, str_, ocean = pl.pallas_call(
-        write_out,
-        out_shape=shapes,
-        in_specs=[vmem_spec] * 3,
-        out_specs=[any_spec] * 3,
-        scratch_shapes=[dma((3,))],
-        compiler_params=pltpu.CompilerParams(vmem_limit_bytes=8 * 1024 * 1024),
-    )(*results)
     return (
         from_tiles(vel, cols, height),
         from_tiles(str_, cols, height),

time: 32 us -> 30.5 us (0.953)
  local copies, waits for them, and re-layouts: 4.83 us -> 3.52 us
    unnamed x10 -> x7, local copies, waits for them, and re-layouts: 4.83 us -> 3.52 us
    pallas_call x2 -> x1, Pallas kernels: 26.2 us -> 26.1 us  [on_device(): pl.pallas_call(functools.partial(kernel, n_gx, n_gy), out_shape=[jax.Shap...]
where the time goes in v2:
time: 30.5 us; the launch traced here: 30.3 us
  Pallas kernels  26.1 us (86%)
  local copies, waits for them, and re-layouts  3.52 us (12%)
  between operations  0.65 us (2%)
    pallas_call x1, Pallas kernels, on_device(): pl.pallas_call(functools.partial(kernel, n_gx, n_gy), out_shape=[jax.Shap...  26.1 us
    unnamed x7, local copies, waits for them, and re-layouts  3.52 us

profile of v2, /device:TPU:1, one launch (start us, length us, event | category | flops | bytes accessed | tf_op | source)
XLA Modules:
  0.0 30.3 jit_solution(6864440154226866968)
XLA Ops:
  0.6 26.1 %shard_map.76 = (f32[2,2,128,128]{3,2,1,0:T(8,128)}, f32[3,2,128,128]{3,2,1,0:T(8,128)}, f32[2,2,128,128]{3,2,1,0:T(8,128)}) custom-call(f32[4,2,128,128]{3,2,1,0:T(8,128)} %bitcast.40, f32[2,2,128,128]{3,2,1,0:T(8,128)} %bitcast.45, f32[2,2,128,128]{3,2,1,0:T(8,128)} %bitcast.46, f32[3,2,128,128]{3,2,1,0:T(8,128)} %bitcast.42, s32[2,128,128]{2,1,0:T(8,128)} %bitcast.47), custom_call_target="tpu_custom_call" | custom-call | tf_op jit(solution)/shard_map/pallas_call | solution.py:578
  26.8 0.0 copy-start
  26.8 1.7 %copy.11 = f32[2,16,2048]{2,1,0:T(8,128)} copy(f32[2,16,2048]{2,1,0:T(8,128)} %bitcast.44) | data formatting | bytes 524288
  28.5 0.0 copy-done
  28.5 0.0 copy-start.1
  28.5 0.7 %copy.12 = f32[3,16,2048]{2,1,0:T(8,128)} copy(f32[3,16,2048]{2,1,0:T(8,128)S(1)} %bitcast.41) | data formatting | bytes 786432
  29.3 0.3 %copy-done.1 = f32[2,2,128,128]{3,2,1,0:T(8,128)S(1)} copy-done((f32[2,2,128,128]{3,2,1,0:T(8,128)S(1)}, f32[2,2,128,128]{3,2,1,0:T(8,128)}, u32[]{:S(2)}) %copy-start.1) | copy-done | bytes 262168
  29.6 0.7 %copy.13 = f32[2,16,2048]{2,1,0:T(8,128)} copy(f32[2,16,2048]{2,1,0:T(8,128)S(1)} %bitcast.43) | data formatting | bytes 524288
Async XLA Ops:
  26.8 1.7 %copy-start = (f32[3,2,128,128]{3,2,1,0:T(8,128)S(1)}, f32[3,2,128,128]{3,2,1,0:T(8,128)}, u32[]{:S(2)}) copy-start(f32[3,2,128,128]{3,2,1,0:T(8,128)} %get-tuple-element.7) | copy-start | bytes 1179652
  28.5 1.1 %copy-start.1 = (f32[2,2,128,128]{3,2,1,0:T(8,128)S(1)}, f32[2,2,128,128]{3,2,1,0:T(8,128)}, u32[]{:S(2)}) copy-start(f32[2,2,128,128]{3,2,1,0:T(8,128)} %get-tuple-element.8) | copy-start | bytes 786436
